TPU v7x, 32 devices: a whole 2x2x4 slice. The times are simulated.
32 devices in a mesh: dp: 2 (over x), ep: 16 (over z, y, core).
Axes of the slice: x: 2, y: 2, z: 4, core: 2. Of those that a mesh axis runs over, the one named last changes fastest.
Arguments:
- x_in: bfloat16 [1024, 2048], P(('dp', 'ep')), parts along dimension 0
- expert_ids: int32 [1024, 8], P(('dp', 'ep')), parts along dimension 0
- norm_weight: bfloat16 [2048], replicated
- router_w: bfloat16 [2048, 64], replicated
- router_b: bfloat16 [64], replicated
- w_gate_up: bfloat16 [64, 2048, 2048], P('ep')
- b_gate_up: bfloat16 [64, 2048], P('ep')
- w_down: bfloat16 [64, 1024, 2048], P('ep')
- b_down: bfloat16 [64, 2048], P('ep')
Outputs:
- output: bfloat16 [1024, 2048], P(('dp', 'ep')), parts along dimension 0
There are 2 independent parts. A program takes and returns all parts, laid end to end along the dimension named above; an argument that names none is the same for every part.
All inputs are finite; a program needn't handle non-finite values.
Results may differ from a plain program's by a relative error of at most 0.0063795.
Values are sent between devices in bfloat16 or wider.
A program may use at most 1 GiB of HBM per device.

v0:
```python
import jax
import jax.numpy as jnp
from jax import lax
from jax.sharding import PartitionSpec as P

CAPACITY_FACTOR = 4
EPSILON = 1e-5
LIMIT = 7.0
ALPHA = 1.702


def rms_norm(x_in, norm_weight):
    x_float = x_in.astype(jnp.float32)
    inv_rms = lax.rsqrt(jnp.mean(x_float * x_float, axis=-1, keepdims=True) + EPSILON)
    return (x_float * inv_rms * norm_weight.astype(jnp.float32)).astype(jnp.bfloat16)


def route_gates(hidden, expert_ids, router_w, router_b):
    logits = jnp.dot(hidden, router_w, preferred_element_type=jnp.float32) + router_b.astype(jnp.float32)
    return jax.nn.softmax(jnp.take_along_axis(logits, expert_ids, axis=1), axis=-1)


def clamped_glu(gate_up):
    gate = jnp.minimum(gate_up[..., 0::2].astype(jnp.float32), LIMIT)
    linear = jnp.clip(gate_up[..., 1::2].astype(jnp.float32), -LIMIT, LIMIT)
    return (gate * jax.nn.sigmoid(ALPHA * gate) * (linear + 1.0)).astype(jnp.bfloat16)


def slot_tables(flat_ids, experts, capacity):
    pairs = flat_ids.shape[0]
    onehot = (flat_ids[:, None] == jnp.arange(experts, dtype=jnp.int32)[None, :]).astype(jnp.int32)
    rank = jnp.sum((jnp.cumsum(onehot, axis=0) - 1) * onehot, axis=1)
    slot_pair = jnp.zeros((experts * capacity,), jnp.int32).at[flat_ids * capacity + rank].set(jnp.arange(pairs, dtype=jnp.int32))
    return slot_pair, rank, jnp.sum(onehot, axis=0)


def mix_residual(x_in, gates, picked):
    mixed = jnp.sum(gates[:, :, None] * picked.astype(jnp.float32), axis=1)
    return (x_in.astype(jnp.float32) + mixed).astype(jnp.bfloat16)


def solution(mesh):
    n_group = mesh.shape['ep']
    rows_spec = P(('dp', 'ep'), None)

    def local_block(x_in, expert_ids, norm_weight, router_w, router_b, w_gate_up, b_gate_up, w_down, b_down):
        tok_dev, d_model = x_in.shape
        top_k = expert_ids.shape[1]
        local_exp = w_gate_up.shape[0]
        experts = local_exp * n_group
        capacity = CAPACITY_FACTOR * top_k * tok_dev // experts
        hidden = rms_norm(x_in, norm_weight)
        gates = route_gates(hidden, expert_ids, router_w, router_b)
        flat_ids = expert_ids.reshape(-1)
        slot_pair, rank, _ = slot_tables(flat_ids, experts, capacity)
        rows = jnp.take(hidden, slot_pair // top_k, axis=0).reshape(n_group, local_exp, capacity, d_model)
        received = lax.all_to_all(rows, 'ep', 0, 0, tiled=True)
        gate_up = (jnp.einsum('sgcd,gdf->gscf', received, w_gate_up, preferred_element_type=jnp.float32) + b_gate_up[:, None, None, :].astype(jnp.float32)).astype(jnp.bfloat16)
        expert_out = (jnp.einsum('gscf,gfd->gscd', clamped_glu(gate_up), w_down, preferred_element_type=jnp.float32) + b_down[:, None, None, :].astype(jnp.float32)).astype(jnp.bfloat16)
        returned = lax.all_to_all(expert_out, 'ep', 1, 1, tiled=True)
        back_slot = ((flat_ids % local_exp) * n_group + flat_ids // local_exp) * capacity + rank
        picked = jnp.take(returned.reshape(-1, d_model), back_slot, axis=0).reshape(tok_dev, top_k, d_model)
        return mix_residual(x_in, gates, picked)

    return jax.shard_map(local_block, mesh=mesh, in_specs=(rows_spec, rows_spec, P(), P(), P(), P('ep', None, None), P('ep', None), P('ep', None, None), P('ep', None)), out_specs=rows_spec, check_vma=False)
```

profile of v0, /device:TPU:15, one launch (start us, length us, event | category | flops | bytes accessed | tf_op | source)
XLA Modules:
  0.0 403.4 jit_solution(13353216944410669874)
XLA Ops:
  0.0 0.0 copy-start
  0.0 0.8 copy.24
  0.8 0.1 reshape.243
  0.9 0.1 reshape.245
  1.0 0.1 eq.28
  1.1 0.6 reduce-window.6
  1.7 0.2 slice_reduce_fusion
  1.9 0.1 fusion.20
  2.1 1.4 scatter_custom_fusion
  3.5 1.0 fusion.15
  4.6 0.7 convert_element_type.48
  5.3 0.1 broadcast_in_dim.44
  5.4 1.0 fusion.17
  6.4 6.0 %gather_fusion = bf16[1024,2048]{1,0:T(8,128)(2,1)} fusion(bf16[32,2048]{1,0:T(8,128)(2,1)S(1)} %fusion.17, s32[1024]{0:T(1024)S(1)} %broadcast_clamp_fusion), kind=kCustom, calls=%fused_computation | custom fusion | bytes 8392704 | tf_op jit(solution)/shard_map/jit(_take)/gather | solution.py:56
  12.4 4.6 %broadcast_select_fusion = bf16[16,4,16,2048]{3,2,1,0:T(8,128)(2,1)} fusion(bf16[16,4,16,2048]{3,2,1,0:T(8,128)(2,1)} %bitcast.46, pred[16,4,16]{2,1,0:T(4,128)(4,1)S(1)} %broadcast_in_dim.44), kind=kLoop, calls=%fused_computation.12 | loop fusion | flops 2097152 | bytes 8389632 | tf_op jit(solution)/shard_map/jit(_take)/select_n | solution.py:56
  17.0 0.0 copy-start.2
  17.0 0.0 copy-start.3
  17.0 6.7 %all-to-all-start = ((bf16[16,4,16,2048]{3,2,1,0:T(8,128)(2,1)}), bf16[16,4,16,2048]{3,2,1,0:T(8,128)(2,1)}, u32[]{:S(2)}, u32[]{:S(2)}) async-start(bf16[16,4,16,2048]{3,2,1,0:T(8,128)(2,1)} %broadcast_select_fusion), calls=%async_computation | async-start | bytes 8388608 | tf_op jit(solution)/shard_map/all_to_all | solution.py:57
  23.7 0.0 copy-done.2
  23.7 0.0 copy-done.3
  23.7 92.6 %all-to-all-done = bf16[16,4,16,2048]{3,2,1,0:T(8,128)(2,1)} async-done(((bf16[16,4,16,2048]{3,2,1,0:T(8,128)(2,1)}), bf16[16,4,16,2048]{3,2,1,0:T(8,128)(2,1)}, u32[]{:S(2)}, u32[]{:S(2)}) %all-to-all-start) | async-done | bytes 4194336 | tf_op jit(solution)/shard_map/all_to_all | solution.py:57
  116.3 17.7 %add_convert_fusion.1 = bf16[4,16,16,2048]{3,2,1,0:T(8,128)(2,1)} fusion(f32[4,2048]{1,0:T(4,128)S(1)} %convert_element_type.52, bf16[4,2048,2048]{2,1,0:T(8,128)(2,1)} %param.14, bf16[16,4,16,2048]{3,2,1,0:T(8,128)(2,1)} %all-to-all-done), kind=kOutput, calls=%fused_computation.9 | convolution fusion | flops 8594128896 | bytes 41975808 | tf_op jit(solution)/shard_map/sgcd,gdf->gscf/dot_general | solution.py:58
  134.0 72.4 %slice.15 = bf16[4,16,16,1024]{3,2,1,0:T(8,128)(2,1)S(1)} slice(bf16[4,16,16,2048]{3,2,1,0:T(8,128)(2,1)} %add_convert_fusion.1), slice={[0:4:1], [0:16:1], [0:16:1], [1:2048:2]} | slice | bytes 4194304 | tf_op jit(solution)/shard_map/slice | solution.py:25
  206.4 73.1 %slice.14 = bf16[4,16,16,1024]{3,2,1,0:T(8,128)(2,1)} slice(bf16[4,16,16,2048]{3,2,1,0:T(8,128)(2,1)} %add_convert_fusion.1), slice={[0:4:1], [0:16:1], [0:16:1], [0:2048:2]} | slice | bytes 4194304 | tf_op jit(solution)/shard_map/slice | solution.py:24
  279.5 11.6 %add_convert_fusion = bf16[4,16,16,2048]{3,2,1,0:T(8,128)(2,1)S(1)} fusion(f32[4,2048]{1,0:T(4,128)S(1)} %convert_element_type.57, bf16[4,1024,2048]{2,1,0:T(8,128)(2,1)} %param.16, bf16[4,16,16,1024]{3,2,1,0:T(8,128)(2,1)S(1)} %slice.15, bf16[4,16,16,1024]{3,2,1,0:T(8,128)(2,1)} %slice.14), kind=kOutput, calls=%fused_computation.8 | convolution fusion | flops 4311744512 | bytes 25198592 | tf_op jit(solution)/shard_map/gscf,gfd->gscd/dot_general | solution.py:59
  291.1 2.6 copy.35
  293.7 0.0 copy-start.4
  293.7 4.9 %all-to-all-start.1 = ((bf16[4,16,16,2048]{3,2,0,1:T(8,128)(2,1)}), bf16[4,16,16,2048]{3,2,0,1:T(8,128)(2,1)}, u32[]{:S(2)}, u32[]{:S(2)}) async-start(bf16[4,16,16,2048]{3,2,0,1:T(8,128)(2,1)} %copy.35), calls=%async_computation.1 | async-start | bytes 8388608 | tf_op jit(solution)/shard_map/all_to_all | solution.py:60
  298.6 0.1 reduce_sum.43
  298.7 0.0 copy-done.4
  298.7 0.1 reshape.263
  298.8 0.0 copy-done
  298.8 0.2 convolution_add_fusion
  299.0 2.0 gather_fusion.2
  301.0 0.1 reshape.266
  301.1 0.1 fusion.42
  301.2 0.2 fusion.31
  301.4 0.1 fusion.30
  301.5 89.8 %all-to-all-done.1 = bf16[4,16,16,2048]{3,2,0,1:T(8,128)(2,1)} async-done(((bf16[4,16,16,2048]{3,2,0,1:T(8,128)(2,1)}), bf16[4,16,16,2048]{3,2,0,1:T(8,128)(2,1)}, u32[]{:S(2)}, u32[]{:S(2)}) %all-to-all-start.1) | async-done | bytes 4194336 | tf_op jit(solution)/shard_map/all_to_all | solution.py:60
  391.3 4.7 %copy.36 = bf16[4,16,16,2048]{3,2,1,0:T(8,128)(2,1)} copy(bf16[4,16,16,2048]{3,2,0,1:T(8,128)(2,1)} %all-to-all-done.1) | data formatting | bytes 8388608 | tf_op jit(solution)/shard_map/all_to_all | solution.py:60
  396.0 0.0 copy-start.1
  396.0 5.1 %gather_fusion.1 = bf16[256,2048]{1,0:T(8,128)(2,1)S(1)} fusion(bf16[1024,2048]{1,0:T(8,128)(2,1)} %bitcast.45, s32[1024]{0:T(1024)S(1)} %pad_clamp_fusion), kind=kCustom, calls=%fused_computation.1 | custom fusion | bytes 2098176 | tf_op jit(solution)/shard_map/jit(_take)/gather | solution.py:62
  401.1 1.6 multiply_reduce_fusion
  402.7 0.0 copy-done.1
  402.7 0.7 fusion.18
  (14 shorter events, 0.2 us)
Async XLA Ops:
  0.0 298.8 %copy-start = (bf16[2048,64]{0,1:T(8,128)(2,1)S(1)}, bf16[2048,64]{0,1:T(8,128)(2,1)}, u32[]{:S(2)}) copy-start(bf16[2048,64]{0,1:T(8,128)(2,1)} %param.12) | copy-start | bytes 786436
  17.0 6.7 %copy-start.2 = (bf16[4,2048]{1,0:T(4,128)(2,1)S(1)}, bf16[4,2048]{1,0:T(4,128)(2,1)}, u32[]{:S(2)}) copy-start(bf16[4,2048]{1,0:T(4,128)(2,1)} %param.15) | copy-start | bytes 49156
  17.0 6.7 %copy-start.3 = (bf16[4,2048]{1,0:T(4,128)(2,1)S(1)}, bf16[4,2048]{1,0:T(4,128)(2,1)}, u32[]{:S(2)}) copy-start(bf16[4,2048]{1,0:T(4,128)(2,1)} %param.17) | copy-start | bytes 49156
  17.0 99.3 %all-to-all-start = ((bf16[16,4,16,2048]{3,2,1,0:T(8,128)(2,1)}), bf16[16,4,16,2048]{3,2,1,0:T(8,128)(2,1)}, u32[]{:S(2)}, u32[]{:S(2)}) async-start(bf16[16,4,16,2048]{3,2,1,0:T(8,128)(2,1)} %broadcast_select_fusion), calls=%async_computation | async-start | bytes 8388608 | tf_op jit(solution)/shard_map/all_to_all | solution.py:57
  293.7 5.0 %copy-start.4 = (bf16[64]{0:T(256)(128)(2,1)S(1)}, bf16[64]{0:T(256)(128)(2,1)}, u32[]{:S(2)}) copy-start(bf16[64]{0:T(256)(128)(2,1)} %param.13) | copy-start | bytes 388
  293.7 97.6 %all-to-all-start.1 = ((bf16[4,16,16,2048]{3,2,0,1:T(8,128)(2,1)}), bf16[4,16,16,2048]{3,2,0,1:T(8,128)(2,1)}, u32[]{:S(2)}, u32[]{:S(2)}) async-start(bf16[4,16,16,2048]{3,2,0,1:T(8,128)(2,1)} %copy.35), calls=%async_computation.1 | async-start | bytes 8388608 | tf_op jit(solution)/shard_map/all_to_all | solution.py:60
  396.0 6.7 %copy-start.1 = (bf16[32,2048]{1,0:T(8,128)(2,1)S(1)}, bf16[32,2048]{1,0:T(8,128)(2,1)}, u32[]{:S(2)}) copy-start(bf16[32,2048]{1,0:T(8,128)(2,1)} %param.9) | copy-start | bytes 393220
where the time goes:
time: 404 us; the launch traced here: 403 us
  waiting for transfers between devices  182 us (45%)
  local copies, waits for them, and re-layouts  169 us (42%)
  matrix products  29.5 us (7%)
  starting transfers between devices  11.6 us (3%)
  other arithmetic  10.9 us (3%)
    all_to_all x1, waiting for transfers between devices, local_block(): received = lax.all_to_all(rows, 'ep', 0, 0, tiled=True)  92.6 us
    all_to_all x1, waiting for transfers between devices, local_block(): returned = lax.all_to_all(expert_out, 'ep', 1, 1, tiled=True)  89.8 us
    slice x1, local copies, waits for them, and re-layouts, clamped_glu(): gate = jnp.minimum(gate_up[..., 0::2].astype(jnp.float32), LIMIT)  73.1 us
    slice x1, local copies, waits for them, and re-layouts, clamped_glu(): linear = jnp.clip(gate_up[..., 1::2].astype(jnp.float32), -LIMIT, LIMIT)  72.4 us
    dot_general x1, matrix products, local_block(): jnp.einsum('sgcd,gdf->gscf', received, w_gate_up, preferred_element_type=...  17.7 us
    dot_general x1, matrix products, local_block(): jnp.einsum('gscf,gfd->gscd', clamped_glu(gate_up), w_down, preferred_elem...  11.6 us
  transfers between devices with their start and end apart: 2, of which 2 were waited for; matrix products, arithmetic and copies ran while one was open for 1% of the time, Pallas kernels for 0%

commit v1 on v0

v1 whole, which is shorter than its diff:
```python
import jax
import jax.numpy as jnp
from jax import lax
from jax.sharding import PartitionSpec as P

CAPACITY_FACTOR = 4
EPSILON = 1e-5
LIMIT = 7.0
ALPHA = 1.702


def rms_norm(x_in, norm_weight):
    x_float = x_in.astype(jnp.float32)
    inv_rms = lax.rsqrt(jnp.mean(x_float * x_float, axis=-1, keepdims=True) + EPSILON)
    return (x_float * inv_rms * norm_weight.astype(jnp.float32)).astype(jnp.bfloat16)


def dense_gates(hidden, expert_ids, router_w, router_b):
    logits = jnp.dot(hidden, router_w, preferred_element_type=jnp.float32) + router_b.astype(jnp.float32)
    experts = router_w.shape[1]
    chosen = jnp.any(expert_ids[:, :, None] == jnp.arange(experts, dtype=jnp.int32)[None, None, :], axis=1)
    top = jnp.max(jnp.where(chosen, logits, -jnp.inf), axis=-1, keepdims=True)
    weight = jnp.where(chosen, jnp.exp(logits - top), 0.0)
    return jnp.where(chosen, weight / jnp.sum(weight, axis=-1, keepdims=True), -1.0)


def solution(mesh):
    n_group = mesh.shape['ep']
    rows_spec = P(('dp', 'ep'), None)

    def local_block(x_in, expert_ids, norm_weight, router_w, router_b, w_gate_up, b_gate_up, w_down, b_down):
        tok_dev, d_model = x_in.shape
        top_k = expert_ids.shape[1]
        local_exp = w_gate_up.shape[0]
        experts = local_exp * n_group
        d_ff = w_down.shape[1]
        capacity = CAPACITY_FACTOR * top_k * tok_dev // experts
        hidden = rms_norm(x_in, norm_weight)
        gates = dense_gates(hidden, expert_ids, router_w, router_b)
        tokens = n_group * tok_dev
        slots = n_group * capacity
        h_all = lax.all_gather(hidden, 'ep', axis=0, tiled=True)
        g_all = lax.all_gather(gates, 'ep', axis=0, tiled=True)
        g_loc = lax.dynamic_slice(g_all, (0, lax.axis_index('ep') * local_exp), (tokens, local_exp))
        mask = (g_loc >= 0).reshape(n_group, tok_dev, local_exp)
        rank = jnp.cumsum(mask.astype(jnp.int32), axis=1) - 1
        slot = rank + (jnp.arange(n_group, dtype=jnp.int32) * capacity)[:, None, None]
        slot = jnp.where(mask, slot, -1).reshape(tokens, local_exp).T
        onehot = (slot[:, None, :] == jnp.arange(slots, dtype=jnp.int32)[None, :, None]).astype(jnp.bfloat16)
        rows = jnp.einsum('est,td->esd', onehot, h_all, preferred_element_type=jnp.float32).astype(jnp.bfloat16)
        u = (jnp.einsum('esd,edf->esf', rows, w_gate_up, preferred_element_type=jnp.float32) + b_gate_up[:, None, :].astype(jnp.float32)).astype(jnp.bfloat16)
        i = jnp.arange(256)
        perm = ((i[:, None] // 2 + 128 * (i[:, None] % 2)) == i[None, :]).astype(jnp.bfloat16)
        v = jnp.einsum('esbi,ij->esbj', u.reshape(local_exp, slots, -1, 256), perm, preferred_element_type=jnp.float32)
        a = jnp.minimum(v[..., :128], LIMIT)
        l = jnp.clip(v[..., 128:], -LIMIT, LIMIT)
        z = (a * jax.nn.sigmoid(ALPHA * a) * (l + 1.0)).astype(jnp.bfloat16).reshape(local_exp, slots, d_ff)
        y = (jnp.einsum('esf,efd->esd', z, w_down, preferred_element_type=jnp.float32) + b_down[:, None, :].astype(jnp.float32)).astype(jnp.bfloat16)
        back = jnp.einsum('est,esd->etd', onehot, y, preferred_element_type=jnp.float32)
        part = jnp.sum(jnp.maximum(g_loc, 0.0).T[:, :, None] * back, axis=0)
        mixed = lax.psum_scatter(part, 'ep', scatter_dimension=0, tiled=True)
        return (x_in.astype(jnp.float32) + mixed).astype(jnp.bfloat16)

    return jax.shard_map(local_block, mesh=mesh, in_specs=(rows_spec, rows_spec, P(), P(), P(), P('ep', None, None), P('ep', None), P('ep', None, None), P('ep', None)), out_specs=rows_spec, check_vma=False)
```

time: 404 us -> 173 us (0.43)
  the two profiles are of different devices: /device:TPU:15 before, /device:TPU:0 now
where the time goes in v1:
time: 173 us; the launch traced here: 172 us
  waiting for transfers between devices  87.6 us (51%)
  matrix products  36.9 us (21%)
  blocking collectives  24 us (14%)
  between operations  13.5 us (8%)
  other arithmetic  9.03 us (5%)
    reduce_scatter x1, waiting for transfers between devices, local_block(): mixed = lax.psum_scatter(part, 'ep', scatter_dimension=0, tiled=True)  71.7 us
    all_gather x1, blocking collectives, local_block(): g_all = lax.all_gather(gates, 'ep', axis=0, tiled=True)  24 us
    dot_general x1, matrix products, local_block(): jnp.einsum('esd,edf->esf', rows, w_gate_up, preferred_element_type=jnp.fl...  19.1 us
    all_gather x1, waiting for transfers between devices, local_block(): h_all = lax.all_gather(hidden, 'ep', axis=0, tiled=True)  15.9 us
    dot_general x1, matrix products, local_block(): jnp.einsum('est,esd->etd', onehot, y, preferred_element_type=jnp.float32)  13.1 us
    dot_general x1, matrix products, local_block(): jnp.einsum('esbi,ij->esbj', u.reshape(local_exp, slots, -1, 256), perm, p...  3.48 us
  transfers between devices with their start and end apart: 2, of which 2 were waited for; matrix products, arithmetic and copies ran while one was open for 3% of the time, Pallas kernels for 0%

profile of v1, /device:TPU:0, one launch (start us, length us, event | category | flops | bytes accessed | tf_op | source)
XLA Modules:
  0.0 172.3 jit_solution(16053020245657128429)
XLA Ops:
  6.5 0.0 copy-start
  6.5 0.0 copy-start.3
  6.5 0.0 all-gather.2.cloned.1.call-start
  6.5 0.7 convert_element_type.45
  7.3 1.0 fusion.17
  8.3 1.7 fusion.19
  10.0 0.0 all-gather.2.cloned.1.call-update
  10.0 0.0 reduce-scatter.2.cloned.1.call-start
  10.1 0.8 copy.16
  10.8 0.7 convert_element_type.47
  11.5 0.1 fusion.26
  11.6 0.0 copy-done
  11.6 1.2 select_reduce_fusion
  12.8 0.2 fusion.27
  13.0 0.1 divide_select_fusion
  13.1 24.0 %all_gather.6 = f32[512,64]{1,0:T(8,128)S(1)} all-gather(f32[32,64]{1,0:T(8,128)S(1)} %divide_select_fusion), channel_id=1, replica_groups=mesh['dp'=2,'ep'=16] {'ep'}, dimensions={0}, use_global_device_ids=true | all-gather | bytes 139264 | tf_op jit(solution)/shard_map/all_gather | solution.py:43
  37.2 0.1 maximum_bitcast_fusion
  37.3 0.1 copy.17
  37.4 0.7 convert_element_type.51
  38.2 0.1 fusion.32
  38.3 0.2 reduce-window_add_fusion
  38.5 0.1 copy.19
  38.6 0.1 add.95
  38.7 0.1 add.96
  38.7 0.1 fusion.21
  38.9 0.1 copy.20
  39.0 0.0 copy-done.3
  39.0 15.9 %all-gather.2.cloned.1.call-done = bf16[512,2048]{1,0:T(8,128)(2,1)} async-done(((bf16[32,2048]{1,0:T(8,128)(2,1)}), bf16[512,2048]{1,0:T(8,128)(2,1)}) %all-gather.2.cloned.1.call-update) | async-done | bytes 2097168 | tf_op jit(solution)/shard_map/all_gather | solution.py:42
  54.9 19.1 %add_convert_fusion.1 = bf16[4,256,2048]{2,1,0:T(8,128)(2,1)} fusion(f32[4,2048]{1,0:T(4,128)S(1)} %convert_element_type.51, bf16[4,2048,2048]{2,1,0:T(8,128)(2,1)} %param.14, bf16[512,2048]{1,0:T(8,128)(2,1)} %all-gather.2.cloned.1.call-done, s32[4,512]{1,0:T(4,128)S(1)} %copy.20), kind=kOutput, calls=%fused_computation.2 | convolution fusion | flops 10742136832 | bytes 39886848 | tf_op jit(solution)/shard_map/esd,edf->esf/dot_general | solution.py:51
  74.0 3.5 %fusion.2 = f32[4,256,8,256]{1,3,2,0:T(8,128)S(1)} fusion(bf16[4,32,8,8,256]{4,3,2,1,0:T(8,128)(2,1)} %bitcast.31, s32[256]{0:T(256)S(1)} %fusion.31), kind=kOutput, calls=%fused_computation.4 | convolution fusion | flops 1073807360 | bytes 12583936 | tf_op jit(solution)/shard_map/esbi,ij->esbj/dot_general | solution.py:54
  77.5 1.6 fusion.7
  79.1 0.0 copy-start.1
  79.1 13.1 %multiply_reduce_fusion = f32[512,2048]{1,0:T(8,128)} fusion(f32[4,512]{1,0:T(4,128)S(1)} %copy.17, bf16[4,256,1024]{1,2,0:T(8,128)(2,1)S(1)} %bitcast.32, bf16[4,1024,2048]{2,1,0:T(8,128)(2,1)} %param.16, f32[4,2048]{1,0:T(4,128)S(1)} %convert_element_type.54, s32[4,512]{1,0:T(4,128)S(1)} %copy.20), kind=kOutput, calls=%fused_computation | convolution fusion | flops 6454509568 | bytes 23117824 | tf_op jit(solution)/shard_map/est,esd->etd/dot_general | solution.py:59
  92.1 0.0 copy-start.2
  92.1 0.0 reduce-scatter.2.cloned.1.call-update
  92.1 71.7 %reduce-scatter.2.cloned.1.call-done = f32[32,2048]{1,0:T(8,128)} async-done(((f32[512,2048]{1,0:T(8,128)}), f32[32,2048]{1,0:T(8,128)}) %reduce-scatter.2.cloned.1.call-update) | async-done | bytes 262160 | tf_op jit(solution)/shard_map/reduce_scatter | solution.py:61
  163.8 0.0 copy-done.2
  163.8 1.6 fusion.20
  165.4 0.0 copy-done.1
  (4 shorter events, 0.0 us)
Async XLA Ops:
  6.5 5.1 %copy-start = (bf16[2048,64]{0,1:T(8,128)(2,1)S(1)}, bf16[2048,64]{0,1:T(8,128)(2,1)}, u32[]{:S(2)}) copy-start(bf16[2048,64]{0,1:T(8,128)(2,1)} %param.12) | copy-start | bytes 786436
  6.5 32.5 %copy-start.3 = (bf16[4,2048]{1,0:T(4,128)(2,1)S(1)}, bf16[4,2048]{1,0:T(4,128)(2,1)}, u32[]{:S(2)}) copy-start(bf16[4,2048]{1,0:T(4,128)(2,1)} %param.17) | copy-start | bytes 49156
  6.5 48.4 %all-gather.2.cloned.1.call-start = ((), (), s32[]{:S(2)}) async-start(), calls=%async_computation.1 | async-start | bytes 2228224 | tf_op jit(solution)/shard_map/all_gather | solution.py:42
  10.0 153.8 %reduce-scatter.2.cloned.1.call-start = ((), (), s32[]{:S(2)}) async-start(), calls=%async_computation.2 | async-start | bytes 4456448 | tf_op jit(solution)/shard_map/reduce_scatter | solution.py:61
  79.1 86.4 %copy-start.1 = (bf16[2048,64]{0,1:T(8,128)(2,1)S(1)}, bf16[2048,64]{0,1:T(8,128)(2,1)}, u32[]{:S(2)}) copy-start(bf16[2048,64]{0,1:T(8,128)(2,1)} %param.12) | copy-start | bytes 786436
  92.1 71.7 %copy-start.2 = (bf16[32,2048]{1,0:T(8,128)(2,1)S(1)}, bf16[32,2048]{1,0:T(8,128)(2,1)}, u32[]{:S(2)}) copy-start(bf16[32,2048]{1,0:T(8,128)(2,1)} %param.9) | copy-start | bytes 393220
Sparse Core Ops, SparseCore 0:
  10.1 44.7 all-gather.1
  92.3 71.5 reduce-scatter.1

commit v2 on v0

v2 whole, which is shorter than its diff:
```python
import functools

import jax
import jax.numpy as jnp
from jax import lax
from jax.experimental import pallas as pl
from jax.experimental.pallas import tpu as pltpu
from jax.sharding import PartitionSpec as P

CAPACITY_FACTOR = 4
EPSILON = 1e-5
LIMIT = 7.0
ALPHA = 1.702
MESH = pl.DeviceIdType.MESH
PIECES = 4
F32 = jnp.float32
BF16 = jnp.bfloat16


def dot(a, b):
    return jnp.dot(a, b, preferred_element_type=F32)


def iota(shape, dim):
    return lax.broadcasted_iota(jnp.int32, shape, dim)


def moe_kernel(cfg, x_ref, ids_ref, g_ref, wr_ref, br_ref, wgu_hbm, bgu_ref, wd_hbm, bd_ref, out_ref,
               wgu, wd, hid, gate, sel, back, pgate, slot_t, rows, glu, perm, bgu, bd,
               acc, r_core, r_y, r_near, r_mid, r_far,
               s_w, s_h, q_h, s_g, q_g, s_core, q_core, s_y, q_y, s_near, q_near, s_mid, q_mid, s_far, q_far, s_fwd):
    tok, d_model, d_ff, top_k, experts, local_exp, cap = cfg
    tc = 8 * tok
    ns = 8 * cap
    cw = d_model // PIECES
    me = lax.axis_index('ep')
    z, y, c = lax.div(me, 4), lax.rem(lax.div(me, 2), 2), lax.rem(me, 2)
    pair, zin = lax.div(z, 2), lax.rem(z, 2)
    is_mid = zin != pair
    is_end = zin == pair
    partner, ypeer, zpeer, midpeer = me + 1 - 2 * c, me + 2 - 4 * y, me + 4 - 8 * zin, me + 4 - 8 * pair

    def pos(q, cc, yy, zz):
        return ((q * 2 + cc) * 2 + yy) * 2 + zz

    def remote(src, dst, send, recv, dev):
        return pltpu.make_async_remote_copy(src_ref=src, dst_ref=dst, send_sem=send, recv_sem=recv,
                                            device_id={'ep': dev}, device_id_type=MESH)

    def w_copy(i):
        if i < local_exp:
            return pltpu.make_async_copy(wgu_hbm.at[i], wgu.at[i], s_w.at[i])
        return pltpu.make_async_copy(wd_hbm.at[i - local_exp], wd.at[i - local_exp], s_w.at[i])

    for i in range(2 * local_exp):
        w_copy(i).start()

    barrier = pltpu.get_barrier_semaphore()
    for dev in (partner, ypeer, zpeer):
        pl.semaphore_signal(barrier, inc=1, device_id={'ep': dev}, device_id_type=MESH)

    @pl.when(is_mid)
    def _():
        pl.semaphore_signal(barrier, inc=1, device_id={'ep': midpeer}, device_id_type=MESH)

    own = pos(pair, c, y, zin)
    x = x_ref[...].astype(F32)
    inv = lax.rsqrt(jnp.mean(x * x, axis=-1, keepdims=True) + EPSILON)
    h = (x * inv * g_ref[...].astype(F32)).astype(BF16)
    hid[pl.ds(own * tok, tok), :] = h
    logits = dot(h, wr_ref[...]) + br_ref[...].astype(F32)
    lane_e = iota((tok, experts), 1)
    ids = ids_ref[...]
    chosen = ids[:, 0:1] == lane_e
    for k in range(1, top_k):
        chosen = jnp.logical_or(chosen, ids[:, k:k + 1] == lane_e)
    top = jnp.max(jnp.where(chosen, logits, -jnp.inf), axis=-1, keepdims=True)
    weight = jnp.where(chosen, jnp.exp(jnp.where(chosen, logits - top, 0.0)), 0.0)
    gates = jnp.where(chosen, weight / jnp.sum(weight, axis=-1, keepdims=True), -1.0)
    gate[pl.ds(own * tok, tok), :] = jnp.concatenate([gates, jnp.full((tok, 128 - experts), -1.0, F32)], axis=1)

    @pl.when(is_mid)
    def _():
        pl.semaphore_wait(barrier, 4)

    @pl.when(is_end)
    def _():
        pl.semaphore_wait(barrier, 3)

    def block(b, d, dev):
        rs = pl.ds(b * tok, tok)
        return (remote(hid.at[rs], hid.at[rs], s_h.at[d, b], q_h.at[b], dev),
                remote(gate.at[rs], gate.at[rs], s_g.at[d, b], q_g.at[b], dev))

    TO_Z, TO_Y, TO_C, TO_M = 0, 1, 2, 3
    dest = {TO_Z: zpeer, TO_Y: ypeer, TO_C: partner, TO_M: midpeer}

    def send(b, *ds):
        for d in ds:
            for cp in block(b, d, dest[d]):
                cp.start()

    def sent(b, *ds):
        for d in ds:
            for cp in block(b, d, dest[d]):
                cp.wait_send()

    def arrived(b):
        for cp in block(b, 0, zpeer):
            cp.wait_recv()

    near = pos(pair, c, y, 1 - zin)
    y_own, y_near = pos(pair, c, 1 - y, zin), pos(pair, c, 1 - y, 1 - zin)
    far = [pos(1 - pair, c, y, pair), pos(1 - pair, c, y, 1 - pair)]
    y_far = [pos(1 - pair, c, 1 - y, pair), pos(1 - pair, c, 1 - y, 1 - pair)]

    send(own, TO_Z, TO_Y)

    @pl.when(is_mid)
    def _():
        send(own, TO_M)
    send(own, TO_C)

    bgu[...] = bgu_ref[...].astype(F32)
    bd[...] = bd_ref[...].astype(F32)
    pi, pj = iota((256, 256), 0), iota((256, 256), 1)
    perm[...] = (lax.div(pi, 2) + 128 * lax.rem(pi, 2) == pj).astype(F32).astype(BF16)

    arrived(y_own)
    send(y_own, TO_C)
    arrived(near)
    send(near, TO_Y)

    @pl.when(is_mid)
    def _():
        send(near, TO_M)
    send(near, TO_C)
    arrived(y_near)
    send(y_near, TO_C)
    for yy in range(2):
        for zz in range(2):
            arrived(pos(pair, 1 - c, yy, zz))

    def forward_far():
        @pl.when(is_mid)
        def _():
            for b in far:
                arrived(b)
                send(b, TO_Z, TO_Y)
                send(b, TO_C)

    def forward_far_end():
        @pl.when(is_end)
        def _():
            for b in far:
                arrived(b)
                send(b, TO_Y)
                send(b, TO_C)

    def forward_far_y():
        for b in y_far:
            arrived(b)
            send(b, TO_C)

    def finish_far():
        for yy in range(2):
            for zz in range(2):
                arrived(pos(1 - pair, 1 - c, yy, zz))

    def route(q):
        g = gate[pl.ds(q * tc, tc), :]
        hit = g >= 0.0
        ri, rj = iota((tc, tc), 0), iota((tc, tc), 1)
        before = jnp.logical_and(rj < ri, lax.div(rj, tok) == lax.div(ri, tok)).astype(F32).astype(BF16)
        rank = dot(before, hit.astype(F32).astype(BF16))
        base = (lax.div(iota((tc, 128), 0), tok) * cap).astype(F32)
        slot = jnp.where(hit, rank + base, -1.0)
        slot_t[...] = slot.T
        lane = iota((tc, 128), 1)
        s_lane = iota((tc, ns), 1).astype(F32)
        s_row = iota((ns, tc), 0).astype(F32)
        for e in range(local_exp):
            col = me * local_exp + e
            pick = lane == col
            p_e = jnp.sum(jnp.where(pick, jnp.maximum(g, 0.0), 0.0), axis=1, keepdims=True)
            s_e = jnp.sum(jnp.where(pick, slot, 0.0), axis=1, keepdims=True)
            back[:, e * ns:(e + 1) * ns] = (s_e == s_lane).astype(F32).astype(BF16)
            pgate[:, e * 128:(e + 1) * 128] = jnp.broadcast_to(p_e, (tc, 128))
            sel[e * ns:(e + 1) * ns, :] = (slot_t[pl.ds(col, 1), :] == s_row).astype(F32).astype(BF16)

    nb_w = 512
    def gate_up(e, q):
        pick = sel[pl.ds(e * ns, ns), :]
        valid = jnp.max(pick.astype(F32), axis=1, keepdims=True) > 0.0
        for i in range(d_model // nb_w):
            sl = slice(i * nb_w, (i + 1) * nb_w)
            rows[:, sl] = dot(pick, hid[pl.ds(q * tc, tc), sl]).astype(BF16)
        for i in range(2 * d_ff // nb_w):
            sl = slice(i * nb_w, (i + 1) * nb_w)
            u = (dot(rows[...], wgu[e, :, sl]) + bgu[pl.ds(e, 1), sl]).astype(BF16)
            for j in range(nb_w // 256):
                v = dot(u[:, j * 256:(j + 1) * 256], perm[...])
                a = jnp.minimum(v[:, :128], LIMIT)
                l = jnp.clip(v[:, 128:], -LIMIT, LIMIT)
                o = a * jax.nn.sigmoid(ALPHA * a) * (l + 1.0)
                m = i * (nb_w // 256) + j
                glu[e, :, m * 128:(m + 1) * 128] = jnp.where(valid, o, 0.0).astype(BF16)

    def down(n, k):
        cols = pl.ds(pl.multiple_of(n * cw, 128), cw)
        for e in range(local_exp):
            y_e = (dot(glu[e], wd[e, :, cols]) + bd[e:e + 1, cols]).astype(BF16)
            t = dot(back[:, e * ns:(e + 1) * ns], y_e)
            p_e = pgate[:, e * 128:(e + 1) * 128]
            for j in range(cw // 128):
                js = slice(j * 128, (j + 1) * 128)
                if e == 0:
                    acc[k, n, :, js] = p_e * t[:, js]
                else:
                    acc[k, n, :, js] += p_e * t[:, js]

    def core_copy(k, n):
        return remote(acc.at[k, n, pl.ds((1 - c) * 4 * tok, 4 * tok)], r_core.at[k, n], s_core.at[k, n], q_core.at[k, n], partner)

    def y_copy(k, n):
        return remote(acc.at[k, n, pl.ds((c * 2 + 1 - y) * 2 * tok, 2 * tok)], r_y.at[k, n], s_y.at[k, n], q_y.at[k, n], ypeer)

    mine = (c * 2 + y) * 2 * tok

    def near_copy(n):
        return remote(acc.at[0, n, pl.ds(mine + (1 - zin) * tok, tok)], r_near.at[n], s_near.at[n], q_near.at[n], zpeer)

    def mid_copy(n):
        return remote(acc.at[1, n, pl.ds(mine, 2 * tok)], r_mid.at[n], s_mid.at[n], q_mid.at[n], zpeer)

    def far_copy(n):
        return remote(acc.at[1, n, pl.ds(mine, 2 * tok)], r_far.at[n], s_far.at[n], q_far.at[n], midpeer)

    def fwd_copy(n):
        return remote(r_far.at[n, pl.ds((1 - zin) * tok, tok)], r_far.at[n, pl.ds(0, tok)], s_fwd.at[n], q_far.at[n], zpeer)

    def after_core(k, n):
        core_copy(k, n).wait_recv()
        other = pl.ds((1 - y) * 2 * tok, 2 * tok)
        acc[k, n, pl.ds((c * 2 + 1 - y) * 2 * tok, 2 * tok)] += r_core[k, n, other]
        y_copy(k, n).start()
        acc[k, n, pl.ds(mine, 2 * tok)] += r_core[k, n, pl.ds(y * 2 * tok, 2 * tok)]

    def after_y(k, n):
        y_copy(k, n).wait_recv()
        acc[k, n, pl.ds(mine, 2 * tok)] += r_y[k, n]
        if k == 0:
            near_copy(n).start()
        else:
            @pl.when(is_end)
            def _():
                mid_copy(n).start()

    def at_mid(n):
        @pl.when(is_mid)
        def _():
            mid_copy(n).wait_recv()
            acc[1, n, pl.ds(mine, 2 * tok)] += r_mid[n]
            far_copy(n).start()

    def forward(n):
        @pl.when(is_mid)
        def _():
            far_copy(n).wait_recv()
            fwd_copy(n).start()

    def finish(n):
        @pl.when(is_end)
        def _():
            fwd_copy(n).wait_recv()
        near_copy(n).wait_recv()
        cols = slice(n * cw, (n + 1) * cw)
        total = acc[0, n, pl.ds(mine + zin * tok, tok)] + r_near[n]
        total = total + r_far[n, pl.ds(jnp.where(is_mid, zin, 0) * tok, tok)]
        out_ref[:, cols] = (x_ref[:, cols].astype(F32) + total).astype(BF16)

    forward_far()
    route(pair)

    def up0(e, _):
        for i in range(local_exp):
            @pl.when(e == i)
            def _():
                w_copy(i).wait()
        gate_up(e, pair)

        @pl.when(e == 1)
        def _():
            forward_far_end()

        @pl.when(e == 3)
        def _():
            forward_far_y()
        return 0
    lax.fori_loop(0, local_exp, up0, 0)
    for i in range(local_exp, 2 * local_exp):
        w_copy(i).wait()

    def down0(n, _):
        down(n, 0)
        core_copy(0, n).start()

        @pl.when(n > 0)
        def _():
            after_core(0, n - 1)
        return 0
    lax.fori_loop(0, PIECES, down0, 0)

    finish_far()
    route(1 - pair)
    after_core(0, PIECES - 1)

    def up1(e, _):
        gate_up(e, 1 - pair)
        after_y(0, e)
        return 0
    lax.fori_loop(0, local_exp, up1, 0)

    def down1(n, _):
        down(n, 1)
        core_copy(1, n).start()

        @pl.when(n > 0)
        def _():
            after_core(1, n - 1)
        return 0
    lax.fori_loop(0, PIECES, down1, 0)
    after_core(1, PIECES - 1)
    for n in range(PIECES):
        after_y(1, n)
        at_mid(n)
        if n > 0:
            forward(n - 1)
    forward(PIECES - 1)
    for n in range(PIECES):
        finish(n)

    sent(own, TO_Z, TO_Y, TO_C)
    sent(near, TO_Y, TO_C)
    sent(y_own, TO_C)
    sent(y_near, TO_C)
    for b in far:
        sent(b, TO_Y, TO_C)
    for b in y_far:
        sent(b, TO_C)
    for n in range(PIECES):
        for k in range(2):
            core_copy(k, n).wait_send()
            y_copy(k, n).wait_send()
        near_copy(n).wait_send()

    @pl.when(is_mid)
    def _():
        sent(own, TO_M)
        sent(near, TO_M)
        for b in far:
            sent(b, TO_Z)
        for n in range(PIECES):
            far_copy(n).wait_send()
            fwd_copy(n).wait_send()

    @pl.when(is_end)
    def _():
        for n in range(PIECES):
            mid_copy(n).wait_send()


def solution(mesh):
    n_group = mesh.shape['ep']
    rows_spec = P(('dp', 'ep'), None)

    def local_block(x_in, expert_ids, norm_weight, router_w, router_b, w_gate_up, b_gate_up, w_down, b_down):
        tok, d_model = x_in.shape
        top_k = expert_ids.shape[1]
        local_exp, d_ff = w_down.shape[0], w_down.shape[1]
        experts = local_exp * n_group
        cap = CAPACITY_FACTOR * top_k * tok // experts
        cfg = (tok, d_model, d_ff, top_k, experts, local_exp, cap)
        tc, ns, cw = 8 * tok, 8 * cap, d_model // PIECES
        vm = pl.BlockSpec(memory_space=pltpu.VMEM)
        hbm = pl.BlockSpec(memory_space=pl.ANY)
        dma = pltpu.SemaphoreType.DMA
        return pl.pallas_call(
            functools.partial(moe_kernel, cfg),
            out_shape=jax.ShapeDtypeStruct((tok, d_model), BF16),
            in_specs=[vm, vm, vm, vm, vm, hbm, vm, hbm, vm],
            out_specs=vm,
            scratch_shapes=[
                pltpu.VMEM((local_exp, d_model, 2 * d_ff), BF16),
                pltpu.VMEM((local_exp, d_ff, d_model), BF16),
                pltpu.VMEM((n_group * tok, d_model), BF16),
                pltpu.VMEM((n_group * tok, 128), F32),
                pltpu.VMEM((local_exp * ns, tc), BF16),
                pltpu.VMEM((tc, local_exp * ns), BF16),
                pltpu.VMEM((tc, local_exp * 128), F32),
                pltpu.VMEM((128, tc), F32),
                pltpu.VMEM((ns, d_model), BF16),
                pltpu.VMEM((local_exp, ns, d_ff), BF16),
                pltpu.VMEM((256, 256), BF16),
                pltpu.VMEM((local_exp, 2 * d_ff), F32),
                pltpu.VMEM((local_exp, d_model), F32),
                pltpu.VMEM((2, PIECES, tc, cw), F32),
                pltpu.VMEM((2, PIECES, 4 * tok, cw), F32),
                pltpu.VMEM((2, PIECES, 2 * tok, cw), F32),
                pltpu.VMEM((PIECES, tok, cw), F32),
                pltpu.VMEM((PIECES, 2 * tok, cw), F32),
                pltpu.VMEM((PIECES, 2 * tok, cw), F32),
                dma((2 * local_exp,)),
                dma((4, n_group)), dma((n_group,)), dma((4, n_group)), dma((n_group,)),
                dma((2, PIECES)), dma((2, PIECES)), dma((2, PIECES)), dma((2, PIECES)),
                dma((PIECES,)), dma((PIECES,)), dma((PIECES,)), dma((PIECES,)),
                dma((PIECES,)), dma((PIECES,)), dma((PIECES,)),
            ],
            compiler_params=pltpu.CompilerParams(
                collective_id=0, has_side_effects=True, vmem_limit_bytes=67043328),
            name='moe_block',
        )(x_in, expert_ids, norm_weight.reshape(1, -1), router_w, router_b.reshape(1, -1), w_gate_up, b_gate_up, w_down, b_down)

    return jax.shard_map(local_block, mesh=mesh, in_specs=(rows_spec, rows_spec, P(), P(), P(), P('ep', None, None), P('ep', None), P('ep', None, None), P('ep', None)), out_specs=rows_spec, check_vma=False)
```

time: 404 us -> 83.5 us (0.21)
  the two profiles are of different devices: /device:TPU:15 before, /device:TPU:0 now
where the time goes in v2:
time: 83.5 us; the launch traced here: 83.3 us
  Pallas kernels  77.1 us (92%)
  local copies, waits for them, and re-layouts  6.15 us (7%)
    pallas_call x1, Pallas kernels, local_block(): pl.pallas_call(functools.partial(moe_kernel, cfg), out_shape=jax.ShapeDty...  77.1 us
    unnamed x3, local copies, waits for them, and re-layouts  4.88 us

profile of v2, /device:TPU:0, one launch (start us, length us, event | category | flops | bytes accessed | tf_op | source)
XLA Modules:
  0.0 83.3 jit_solution(16593412647120457188)
XLA Ops:
  0.0 1.3 %reshape.6.g_ref = bf16[1,2048]{1,0:T(2,128)(2,1)} reshape(bf16[2048]{0:T(1024)(128)(2,1)} %param.11) | data formatting | bytes 8192 | tf_op jit(solution)/shard_map/reshape | solution.py:422
  1.3 1.4 %copy.10.ids_ref = s32[32,8]{1,0:T(8,128)} copy(s32[32,8]{0,1:T(8,128)} %param.10) | data formatting | bytes 2048 | tf_op args[1]
  2.6 1.9 %copy.11.wr_ref = bf16[2048,64]{1,0:T(8,128)(2,1)} copy(bf16[2048,64]{0,1:T(8,128)(2,1)} %param.12) | data formatting | bytes 524288 | tf_op args[3]
  4.6 77.1 %moe_block.1 = bf16[32,2048]{1,0:T(8,128)(2,1)} custom-call(bf16[32,2048]{1,0:T(8,128)(2,1)} %x_ref.1, s32[32,8]{1,0:T(8,128)} %copy.10.ids_ref, bf16[1,2048]{1,0:T(2,128)(2,1)} %reshape.6.g_ref, bf16[2048,64]{1,0:T(8,128)(2,1)} %copy.11.wr_ref, bf16[1,64]{1,0:T(2,128)(2,1)} %bitcast.1, bf16[4,2048,2048]{2,1,0:T(8,128)(2,1)} %wgu_hbm.1, ...), custom_call_target="tpu_custom_call" | custom-call | tf_op jit(solution)/shard_map/moe_block/pallas_call | solution.py:388
  81.7 1.6 %copy.13 = bf16[32,2048]{1,0:T(8,128)(2,1)} copy(bf16[32,2048]{1,0:T(8,128)(2,1)} %moe_block.1) | data formatting | bytes 262144

commit v3 on v2

v3 whole, which is shorter than its diff:
```python
import functools

import jax
import jax.numpy as jnp
from jax import lax
from jax.experimental import pallas as pl
from jax.experimental.pallas import tpu as pltpu
from jax.sharding import PartitionSpec as P

CAPACITY_FACTOR = 4
EPSILON = 1e-5
LIMIT = 7.0
ALPHA = 1.702
MESH = pl.DeviceIdType.MESH
PIECES = 8
STEPS = 4
F32 = jnp.float32
BF16 = jnp.bfloat16


def dot(a, b):
    return jnp.dot(a, b, preferred_element_type=F32)


def iota(shape, dim):
    return lax.broadcasted_iota(jnp.int32, shape, dim)


def moe_kernel(cfg, x_ref, ids_ref, g_ref, wr_ref, br_ref, wgu_hbm, bgu_ref, wd_hbm, bd_ref, out_ref,
               wgu, wd, hid, gate, sel, back, pgate, slot_t, rows, glu, perm, bgu, bd,
               acc, r_core, r_y, r_z,
               s_w, s_h, q_h, s_g, q_g, s_core, q_core, s_y, q_y, s_z, q_z):
    tok, d_model, d_ff, top_k, experts, local_exp, cap = cfg
    tc = 8 * tok
    ns = 8 * cap
    cw = d_model // PIECES
    half = tok // 2
    me = lax.axis_index('ep')
    z, y, c = lax.div(me, 4), lax.rem(lax.div(me, 2), 2), lax.rem(me, 2)
    pair, zin = lax.div(z, 2), lax.rem(z, 2)
    partner, ypeer, zpeer = me + 1 - 2 * c, me + 2 - 4 * y, me + 4 - 8 * zin
    zfar = [me + 4 * (2 * (1 - pair) + j - z) for j in range(2)]

    def pos(q, cc, yy, zz):
        return ((q * 2 + cc) * 2 + yy) * 2 + zz

    def remote(src, dst, send, recv, dev):
        return pltpu.make_async_remote_copy(src_ref=src, dst_ref=dst, send_sem=send, recv_sem=recv,
                                            device_id={'ep': dev}, device_id_type=MESH)

    def w_copy(i):
        if i < local_exp:
            return pltpu.make_async_copy(wgu_hbm.at[i], wgu.at[i], s_w.at[i])
        return pltpu.make_async_copy(wd_hbm.at[i - local_exp], wd.at[i - local_exp], s_w.at[i])

    for i in range(2 * local_exp):
        w_copy(i).start()

    barrier = pltpu.get_barrier_semaphore()
    for dev in (partner, ypeer, zpeer, *zfar):
        pl.semaphore_signal(barrier, inc=1, device_id={'ep': dev}, device_id_type=MESH)

    own = pos(pair, c, y, zin)
    x = x_ref[...].astype(F32)
    inv = lax.rsqrt(jnp.mean(x * x, axis=-1, keepdims=True) + EPSILON)
    h = (x * inv * g_ref[...].reshape(1, d_model).astype(F32)).astype(BF16)
    hid[pl.ds(own * tok, tok), :] = h
    pl.semaphore_wait(barrier, 5)

    TO_Z, TO_Y, TO_C, TO_F0, TO_F1 = range(5)
    dest = [zpeer, ypeer, partner, zfar[0], zfar[1]]

    def h_copy(b, d, s):
        rs = pl.ds(b * tok + s * half, half)
        return remote(hid.at[rs], hid.at[rs], s_h.at[d, b, s], q_h.at[b, s], dest[d])

    def g_copy(b, d):
        rs = pl.ds(b * tok, tok)
        return remote(gate.at[rs], gate.at[rs], s_g.at[d, b], q_g.at[b], dest[d])

    def send_h(b, s, *ds):
        for d in ds:
            h_copy(b, d, s).start()

    def send_g(b, *ds):
        for d in ds:
            g_copy(b, d).start()

    def pass_h(b, s, *ds):
        h_copy(b, 0, s).wait_recv()
        send_h(b, s, *ds)

    def pass_g(b, *ds):
        g_copy(b, 0).wait_recv()
        send_g(b, *ds)

    def sent(b, *ds):
        for d in ds:
            for s in range(2):
                h_copy(b, d, s).wait_send()
            g_copy(b, d).wait_send()

    near = pos(pair, c, y, 1 - zin)
    y_own, y_near = pos(pair, c, 1 - y, zin), pos(pair, c, 1 - y, 1 - zin)
    far = [pos(1 - pair, c, y, j) for j in range(2)]
    y_far = [pos(1 - pair, c, 1 - y, j) for j in range(2)]

    for s in range(2):
        send_h(own, s, TO_Z, TO_Y)
    for s in range(2):
        send_h(own, s, TO_C)

    logits = lax.dot_general(h, wr_ref[...], (((1,), (1,)), ((), ())), preferred_element_type=F32) + br_ref[...].astype(F32)
    lane_e = iota((tok, experts), 1)
    ids = ids_ref[...].T
    chosen = ids[:, 0:1] == lane_e
    for k in range(1, top_k):
        chosen = jnp.logical_or(chosen, ids[:, k:k + 1] == lane_e)
    top = jnp.max(jnp.where(chosen, logits, -jnp.inf), axis=-1, keepdims=True)
    weight = jnp.where(chosen, jnp.exp(jnp.where(chosen, logits - top, 0.0)), 0.0)
    gates = jnp.where(chosen, weight / jnp.sum(weight, axis=-1, keepdims=True), -1.0)
    gate[pl.ds(own * tok, tok), :] = jnp.concatenate([gates, jnp.full((tok, 128 - experts), -1.0, F32)], axis=1)
    send_g(own, TO_Z, TO_Y, TO_C, TO_F0, TO_F1)
    for s in range(2):
        send_h(own, s, TO_F0, TO_F1)

    bgu[...] = bgu_ref[...].astype(F32)
    bd[...] = bd_ref[...].astype(F32)
    pi, pj = iota((256, 256), 0), iota((256, 256), 1)
    perm[...] = (lax.div(pi, 2) + 128 * lax.rem(pi, 2) == pj).astype(F32).astype(BF16)

    for s in range(2):
        pass_h(near, s, TO_Y, TO_C)
        pass_h(y_own, s, TO_C)
    pass_g(near, TO_Y, TO_C)
    pass_g(y_own, TO_C)
    for s in range(2):
        pass_h(y_near, s, TO_C)
    pass_g(y_near, TO_C)

    def finish_gather(q):
        for yy in range(2):
            for zz in range(2):
                b = pos(q, 1 - c, yy, zz)
                for s in range(2):
                    pass_h(b, s)
                pass_g(b)

    def forward_far():
        for b in far:
            pass_g(b, TO_Y, TO_C)
            for s in range(2):
                pass_h(b, s, TO_Y, TO_C)

    def forward_far_y():
        for b in y_far:
            pass_g(b, TO_C)
            for s in range(2):
                pass_h(b, s, TO_C)

    def route(q):
        g = gate[pl.ds(q * tc, tc), :]
        hit = g >= 0.0
        ri, rj = iota((tc, tc), 0), iota((tc, tc), 1)
        before = jnp.logical_and(rj < ri, lax.div(rj, tok) == lax.div(ri, tok)).astype(F32).astype(BF16)
        rank = dot(before, hit.astype(F32).astype(BF16))
        base = (lax.div(iota((tc, 128), 0), tok) * cap).astype(F32)
        slot = jnp.where(hit, rank + base, -1.0)
        slot_t[...] = slot.T
        lane = iota((tc, 128), 1)
        s_lane = iota((tc, ns), 1).astype(F32)
        s_row = iota((ns, tc), 0).astype(F32)
        for e in range(local_exp):
            col = me * local_exp + e
            pick = lane == col
            p_e = jnp.sum(jnp.where(pick, jnp.maximum(g, 0.0), 0.0), axis=1, keepdims=True)
            s_e = jnp.sum(jnp.where(pick, slot, 0.0), axis=1, keepdims=True)
            back[:, e * ns:(e + 1) * ns] = (s_e == s_lane).astype(F32).astype(BF16)
            pgate[:, e * 128:(e + 1) * 128] = jnp.broadcast_to(p_e, (tc, 128))
            sel[e * ns:(e + 1) * ns, :] = (slot_t[pl.ds(col, 1), :] == s_row).astype(F32).astype(BF16)

    nb_w = 512
    def gate_up(e, q):
        pick = sel[pl.ds(e * ns, ns), :]
        valid = jnp.max(pick.astype(F32), axis=1, keepdims=True) > 0.0
        for i in range(d_model // nb_w):
            sl = slice(i * nb_w, (i + 1) * nb_w)
            rows[:, sl] = dot(pick, hid[pl.ds(q * tc, tc), sl]).astype(BF16)
        for i in range(2 * d_ff // nb_w):
            sl = slice(i * nb_w, (i + 1) * nb_w)
            u = (dot(rows[...], wgu[e, :, sl]) + bgu[pl.ds(e, 1), sl]).astype(BF16)
            for j in range(nb_w // 256):
                v = dot(u[:, j * 256:(j + 1) * 256], perm[...])
                a = jnp.minimum(v[:, :128], LIMIT)
                l = jnp.clip(v[:, 128:], -LIMIT, LIMIT)
                o = a * jax.nn.sigmoid(ALPHA * a) * (l + 1.0)
                m = i * (nb_w // 256) + j
                glu[e, :, m * 128:(m + 1) * 128] = jnp.where(valid, o, 0.0).astype(BF16)

    per = PIECES // STEPS

    def down(n, k):
        cols = pl.ds(pl.multiple_of(n * (per * cw), 128), per * cw)
        for e in range(local_exp):
            y_e = (dot(glu[e], wd[e, :, cols]) + bd[e:e + 1, cols]).astype(BF16)
            t = dot(back[:, e * ns:(e + 1) * ns], y_e)
            p_e = pgate[:, e * 128:(e + 1) * 128]
            for i in range(per):
                for j in range(cw // 128):
                    js = slice(j * 128, (j + 1) * 128)
                    ts = slice(i * cw + j * 128, i * cw + (j + 1) * 128)
                    if e == 0:
                        acc[k, n * per + i, :, js] = p_e * t[:, ts]
                    else:
                        acc[k, n * per + i, :, js] += p_e * t[:, ts]

    mine = (c * 2 + y) * 2 * tok

    def core_copy(k, n):
        return remote(acc.at[k, n, pl.ds((1 - c) * 4 * tok, 4 * tok)], r_core.at[k, n], s_core.at[k, n], q_core.at[k, n], partner)

    def y_copy(k, n):
        return remote(acc.at[k, n, pl.ds((c * 2 + 1 - y) * 2 * tok, 2 * tok)], r_y.at[k, n], s_y.at[k, n], q_y.at[k, n], ypeer)

    def near_copy(n):
        return remote(acc.at[0, n, pl.ds(mine + (1 - zin) * tok, tok)], r_z.at[2, n], s_z.at[2, n], q_z.at[2, n], zpeer)

    def far_copy(j, n):
        return remote(acc.at[1, n, pl.ds(mine + j * tok, tok)], r_z.at[zin, n], s_z.at[j, n], q_z.at[zin, n], zfar[j])

    def far_wait(j, n):
        remote(acc.at[1, n, pl.ds(mine + j * tok, tok)], r_z.at[j, n], s_z.at[j, n], q_z.at[j, n], zfar[j]).wait_recv()

    def start_core(k, n):
        for i in range(per):
            core_copy(k, n * per + i).start()

    def after_core(k, m):
        for i in range(per):
            n = m * per + i
            core_copy(k, n).wait_recv()
            acc[k, n, pl.ds((c * 2 + 1 - y) * 2 * tok, 2 * tok)] += r_core[k, n, pl.ds((1 - y) * 2 * tok, 2 * tok)]
            y_copy(k, n).start()
            acc[k, n, pl.ds(mine, 2 * tok)] += r_core[k, n, pl.ds(y * 2 * tok, 2 * tok)]

    def after_y(k, n):
        y_copy(k, n).wait_recv()
        acc[k, n, pl.ds(mine, 2 * tok)] += r_y[k, n]
        if k == 0:
            near_copy(n).start()
        else:
            for j in range(2):
                far_copy(j, n).start()

    def finish(n):
        near_copy(n).wait_recv()
        for j in range(2):
            far_wait(j, n)
        cols = slice(n * cw, (n + 1) * cw)
        total = acc[0, n, pl.ds(mine + zin * tok, tok)] + r_z[2, n]
        total = total + (r_z[0, n] + r_z[1, n])
        out_ref[:, cols] = (x_ref[:, cols].astype(F32) + total).astype(BF16)

    finish_gather(pair)
    route(pair)

    def up0(e, _):
        for i in range(local_exp):
            @pl.when(e == i)
            def _():
                w_copy(i).wait()
        gate_up(e, pair)

        @pl.when(e == 1)
        def _():
            forward_far()

        @pl.when(e == 3)
        def _():
            forward_far_y()
        return 0
    lax.fori_loop(0, local_exp, up0, 0)
    for i in range(local_exp, 2 * local_exp):
        w_copy(i).wait()

    def down0(n, _):
        down(n, 0)
        start_core(0, n)

        @pl.when(n > 0)
        def _():
            after_core(0, n - 1)
        return 0
    lax.fori_loop(0, STEPS, down0, 0)

    finish_gather(1 - pair)
    after_core(0, STEPS - 1)
    route(1 - pair)

    def up1(e, _):
        gate_up(e, 1 - pair)
        for i in range(per):
            after_y(0, e * per + i)
        return 0
    lax.fori_loop(0, local_exp, up1, 0)

    def down1(n, _):
        down(n, 1)
        start_core(1, n)

        @pl.when(n > 0)
        def _():
            after_core(1, n - 1)
        return 0
    lax.fori_loop(0, STEPS, down1, 0)
    after_core(1, STEPS - 1)
    for n in range(PIECES):
        after_y(1, n)
    for n in range(PIECES):
        finish(n)

    sent(own, TO_Z, TO_Y, TO_C, TO_F0, TO_F1)
    for b in (near, *far):
        sent(b, TO_Y, TO_C)
    for b in (y_own, y_near, *y_far):
        sent(b, TO_C)
    for n in range(PIECES):
        for k in range(2):
            core_copy(k, n).wait_send()
            y_copy(k, n).wait_send()
            far_copy(k, n).wait_send()
        near_copy(n).wait_send()


def solution(mesh):
    n_group = mesh.shape['ep']
    rows_spec = P(('dp', 'ep'), None)

    def local_block(x_in, expert_ids, norm_weight, router_w, router_b, w_gate_up, b_gate_up, w_down, b_down):
        tok, d_model = x_in.shape
        top_k = expert_ids.shape[1]
        local_exp, d_ff = w_down.shape[0], w_down.shape[1]
        experts = local_exp * n_group
        cap = CAPACITY_FACTOR * top_k * tok // experts
        cfg = (tok, d_model, d_ff, top_k, experts, local_exp, cap)
        tc, ns, cw = 8 * tok, 8 * cap, d_model // PIECES
        vm = pl.BlockSpec(memory_space=pltpu.VMEM)
        hbm = pl.BlockSpec(memory_space=pl.ANY)
        dma = pltpu.SemaphoreType.DMA
        return pl.pallas_call(
            functools.partial(moe_kernel, cfg),
            out_shape=jax.ShapeDtypeStruct((tok, d_model), BF16),
            in_specs=[vm, vm, vm, vm, vm, hbm, vm, hbm, vm],
            out_specs=vm,
            scratch_shapes=[
                pltpu.VMEM((local_exp, d_model, 2 * d_ff), BF16),
                pltpu.VMEM((local_exp, d_ff, d_model), BF16),
                pltpu.VMEM((n_group * tok, d_model), BF16),
                pltpu.VMEM((n_group * tok, 128), F32),
                pltpu.VMEM((local_exp * ns, tc), BF16),
                pltpu.VMEM((tc, local_exp * ns), BF16),
                pltpu.VMEM((tc, local_exp * 128), F32),
                pltpu.VMEM((128, tc), F32),
                pltpu.VMEM((ns, d_model), BF16),
                pltpu.VMEM((local_exp, ns, d_ff), BF16),
                pltpu.VMEM((256, 256), BF16),
                pltpu.VMEM((local_exp, 2 * d_ff), F32),
                pltpu.VMEM((local_exp, d_model), F32),
                pltpu.VMEM((2, PIECES, tc, cw), F32),
                pltpu.VMEM((2, PIECES, 4 * tok, cw), F32),
                pltpu.VMEM((2, PIECES, 2 * tok, cw), F32),
                pltpu.VMEM((3, PIECES, tok, cw), F32),
                dma((2 * local_exp,)),
                dma((5, n_group, 2)), dma((n_group, 2)), dma((5, n_group)), dma((n_group,)),
                dma((2, PIECES)), dma((2, PIECES)), dma((2, PIECES)), dma((2, PIECES)),
                dma((3, PIECES)), dma((3, PIECES)),
            ],
            compiler_params=pltpu.CompilerParams(
                collective_id=0, has_side_effects=True, vmem_limit_bytes=67043328),
            name='moe_block',
        )(x_in, expert_ids.T, norm_weight, router_w.T, router_b.reshape(1, -1), w_gate_up, b_gate_up, w_down, b_down)

    return jax.shard_map(local_block, mesh=mesh, in_specs=(rows_spec, rows_spec, P(), P(), P(), P('ep', None, None), P('ep', None), P('ep', None, None), P('ep', None)), out_specs=rows_spec, check_vma=False)
```

time: 83.5 us -> 82.4 us (0.987)
  local copies, waits for them, and re-layouts: 6.15 us -> 1.57 us
  Pallas kernels: 77.1 us -> 80.6 us
    pallas_call x1, Pallas kernels: 77.1 us -> 80.6 us  [local_block(): pl.pallas_call(functools.partial(moe_kernel, cfg), out_shape=jax.ShapeDty...]
    unnamed x3 -> x1, local copies, waits for them, and re-layouts: 4.88 us -> 1.57 us
    reshape x1 -> x0, local copies, waits for them, and re-layouts: 1.27 us -> none  [local_block(): norm_weight.reshape(1, -1)]
where the time goes in v3:
time: 82.4 us; the launch traced here: 82.2 us
  Pallas kernels  80.6 us (98%)
  local copies, waits for them, and re-layouts  1.57 us (2%)
    pallas_call x1, Pallas kernels, local_block(): pl.pallas_call(functools.partial(moe_kernel, cfg), out_shape=jax.ShapeDty...  80.6 us

profile of v3, /device:TPU:0, one launch (start us, length us, event | category | flops | bytes accessed | tf_op | source)
XLA Modules:
  0.0 82.2 jit_solution(8429450729037145628)
XLA Ops:
  0.0 80.6 %moe_block.1 = bf16[32,2048]{1,0:T(8,128)(2,1)} custom-call(bf16[32,2048]{1,0:T(8,128)(2,1)} %x_ref.1, s32[8,32]{1,0:T(8,128)} %bitcast.4, bf16[2048]{0:T(1024)(128)(2,1)} %g_ref.1, bf16[64,2048]{1,0:T(8,128)(2,1)} %bitcast.3, bf16[1,64]{1,0:T(2,128)(2,1)} %bitcast.5, bf16[4,2048,2048]{2,1,0:T(8,128)(2,1)} %wgu_hbm.1, bf16[4,2048]{1,0:T(4,128)(2,1)} %bgu_ref.1, ...), custom_call_target="tpu_custom_call" | custom-call | tf_op jit(solution)/shard_map/moe_block/pallas_call | solution.py:350
  80.7 1.6 %copy.11 = bf16[32,2048]{1,0:T(8,128)(2,1)} copy(bf16[32,2048]{1,0:T(8,128)(2,1)} %moe_block.1) | data formatting | bytes 262144

commit v4 on v3

--- a/solution.py
+++ b/solution.py
@@ -37,9 +37,9 @@
     half = tok // 2
     me = lax.axis_index('ep')
     z, y, c = lax.div(me, 4), lax.rem(lax.div(me, 2), 2), lax.rem(me, 2)
-    pair, zin = lax.div(z, 2), lax.rem(z, 2)
-    partner, ypeer, zpeer = me + 1 - 2 * c, me + 2 - 4 * y, me + 4 - 8 * zin
-    zfar = [me + 4 * (2 * (1 - pair) + j - z) for j in range(2)]
+    pair, zin = lax.rem(z, 2), lax.div(z, 2)
+    partner, ypeer, zpeer = me + 1 - 2 * c, me + 2 - 4 * y, me + 8 - 16 * zin
+    zfar = [me + 4 * (2 * j + 1 - pair - z) for j in range(2)]
 
     def pos(q, cc, yy, zz):
         return ((q * 2 + cc) * 2 + yy) * 2 + zz
@@ -102,8 +102,9 @@
 
     near = pos(pair, c, y, 1 - zin)
     y_own, y_near = pos(pair, c, 1 - y, zin), pos(pair, c, 1 - y, 1 - zin)
-    far = [pos(1 - pair, c, y, j) for j in range(2)]
-    y_far = [pos(1 - pair, c, 1 - y, j) for j in range(2)]
+    first = lax.div(z, 3)
+    far = [pos(1 - pair, c, y, j) for j in (first, 1 - first)]
+    y_far = [pos(1 - pair, c, 1 - y, j) for j in (first, 1 - first)]
 
     for s in range(2):
         send_h(own, s, TO_Z, TO_Y)
@@ -146,17 +147,15 @@
                     pass_h(b, s)
                 pass_g(b)
 
-    def forward_far():
-        for b in far:
-            pass_g(b, TO_Y, TO_C)
-            for s in range(2):
-                pass_h(b, s, TO_Y, TO_C)
-
-    def forward_far_y():
-        for b in y_far:
-            pass_g(b, TO_C)
-            for s in range(2):
-                pass_h(b, s, TO_C)
+    def forward_far(j):
+        pass_g(far[j], TO_Y, TO_C)
+        for s in range(2):
+            pass_h(far[j], s, TO_Y, TO_C)
+
+    def forward_far_y(j):
+        pass_g(y_far[j], TO_C)
+        for s in range(2):
+            pass_h(y_far[j], s, TO_C)
 
     def route(q):
         g = gate[pl.ds(q * tc, tc), :]
@@ -179,40 +178,31 @@
             pgate[:, e * 128:(e + 1) * 128] = jnp.broadcast_to(p_e, (tc, 128))
             sel[e * ns:(e + 1) * ns, :] = (slot_t[pl.ds(col, 1), :] == s_row).astype(F32).astype(BF16)
 
-    nb_w = 512
     def gate_up(e, q):
-        pick = sel[pl.ds(e * ns, ns), :]
+        pick = sel[e * ns:(e + 1) * ns, :]
         valid = jnp.max(pick.astype(F32), axis=1, keepdims=True) > 0.0
-        for i in range(d_model // nb_w):
-            sl = slice(i * nb_w, (i + 1) * nb_w)
-            rows[:, sl] = dot(pick, hid[pl.ds(q * tc, tc), sl]).astype(BF16)
-        for i in range(2 * d_ff // nb_w):
-            sl = slice(i * nb_w, (i + 1) * nb_w)
-            u = (dot(rows[...], wgu[e, :, sl]) + bgu[pl.ds(e, 1), sl]).astype(BF16)
-            for j in range(nb_w // 256):
-                v = dot(u[:, j * 256:(j + 1) * 256], perm[...])
-                a = jnp.minimum(v[:, :128], LIMIT)
-                l = jnp.clip(v[:, 128:], -LIMIT, LIMIT)
-                o = a * jax.nn.sigmoid(ALPHA * a) * (l + 1.0)
-                m = i * (nb_w // 256) + j
-                glu[e, :, m * 128:(m + 1) * 128] = jnp.where(valid, o, 0.0).astype(BF16)
+        rows[...] = dot(pick, hid[pl.ds(q * tc, tc), :]).astype(BF16)
+        u = (dot(rows[...], wgu[e]) + bgu[e:e + 1, :]).astype(BF16)
+        for j in range(2 * d_ff // 256):
+            v = dot(u[:, j * 256:(j + 1) * 256], perm[...])
+            a = jnp.minimum(v[:, :128], LIMIT)
+            l = jnp.clip(v[:, 128:], -LIMIT, LIMIT)
+            o = a * jax.nn.sigmoid(ALPHA * a) * (l + 1.0)
+            glu[e, :, j * 128:(j + 1) * 128] = jnp.where(valid, o, 0.0).astype(BF16)
 
     per = PIECES // STEPS
 
     def down(n, k):
         cols = pl.ds(pl.multiple_of(n * (per * cw), 128), per * cw)
-        for e in range(local_exp):
-            y_e = (dot(glu[e], wd[e, :, cols]) + bd[e:e + 1, cols]).astype(BF16)
-            t = dot(back[:, e * ns:(e + 1) * ns], y_e)
-            p_e = pgate[:, e * 128:(e + 1) * 128]
-            for i in range(per):
-                for j in range(cw // 128):
-                    js = slice(j * 128, (j + 1) * 128)
-                    ts = slice(i * cw + j * 128, i * cw + (j + 1) * 128)
-                    if e == 0:
-                        acc[k, n * per + i, :, js] = p_e * t[:, ts]
-                    else:
-                        acc[k, n * per + i, :, js] += p_e * t[:, ts]
+        ys = [(dot(glu[e], wd[e, :, cols]) + bd[e:e + 1, cols]).astype(BF16) for e in range(local_exp)]
+        ts = [dot(back[:, e * ns:(e + 1) * ns], ys[e]) for e in range(local_exp)]
+        for i in range(per):
+            for j in range(cw // 128):
+                sl = slice(i * cw + j * 128, i * cw + (j + 1) * 128)
+                part = pgate[:, 0:128] * ts[0][:, sl]
+                for e in range(1, local_exp):
+                    part = part + pgate[:, e * 128:(e + 1) * 128] * ts[e][:, sl]
+                acc[k, n * per + i, :, j * 128:(j + 1) * 128] = part
 
     mine = (c * 2 + y) * 2 * tok
 
@@ -264,22 +254,11 @@
     finish_gather(pair)
     route(pair)
 
-    def up0(e, _):
-        for i in range(local_exp):
-            @pl.when(e == i)
-            def _():
-                w_copy(i).wait()
+    for e in range(local_exp):
+        w_copy(e).wait()
         gate_up(e, pair)
-
-        @pl.when(e == 1)
-        def _():
-            forward_far()
-
-        @pl.when(e == 3)
-        def _():
-            forward_far_y()
-        return 0
-    lax.fori_loop(0, local_exp, up0, 0)
+        if e < 2:
+            forward_far(e)
     for i in range(local_exp, 2 * local_exp):
         w_copy(i).wait()
 
@@ -290,19 +269,24 @@
         @pl.when(n > 0)
         def _():
             after_core(0, n - 1)
+
+        @pl.when(n == 1)
+        def _():
+            forward_far_y(0)
+
+        @pl.when(n == 3)
+        def _():
+            forward_far_y(1)
         return 0
     lax.fori_loop(0, STEPS, down0, 0)
 
+    after_core(0, STEPS - 1)
     finish_gather(1 - pair)
-    after_core(0, STEPS - 1)
     route(1 - pair)
-
-    def up1(e, _):
+    for e in range(local_exp):
         gate_up(e, 1 - pair)
         for i in range(per):
             after_y(0, e * per + i)
-        return 0
-    lax.fori_loop(0, local_exp, up1, 0)
 
     def down1(n, _):
         down(n, 1)

time: 82.4 us -> 71.2 us (0.86)
  Pallas kernels: 80.6 us -> 69.5 us
    pallas_call x1, Pallas kernels: 80.6 us -> 69.5 us  [local_block(): pl.pallas_call(functools.partial(moe_kernel, cfg), out_shape=jax.ShapeDty...]
where the time goes in v4:
time: 71.2 us; the launch traced here: 71 us
  Pallas kernels  69.5 us (98%)
  local copies, waits for them, and re-layouts  1.57 us (2%)
    pallas_call x1, Pallas kernels, local_block(): pl.pallas_call(functools.partial(moe_kernel, cfg), out_shape=jax.ShapeDty...  69.5 us
    unnamed x1, local copies, waits for them, and re-layouts  1.57 us

profile of v4, /device:TPU:0, one launch (start us, length us, event | category | flops | bytes accessed | tf_op | source)
XLA Modules:
  0.0 71.0 jit_solution(12833944531733934713)
XLA Ops:
  0.0 69.5 %moe_block.1 = bf16[32,2048]{1,0:T(8,128)(2,1)} custom-call(bf16[32,2048]{1,0:T(8,128)(2,1)} %x_ref.1, s32[8,32]{1,0:T(8,128)} %bitcast.4, bf16[2048]{0:T(1024)(128)(2,1)} %g_ref.1, bf16[64,2048]{1,0:T(8,128)(2,1)} %bitcast.3, bf16[1,64]{1,0:T(2,128)(2,1)} %bitcast.5, bf16[4,2048,2048]{2,1,0:T(8,128)(2,1)} %wgu_hbm.1, bf16[4,2048]{1,0:T(4,128)(2,1)} %bgu_ref.1, ...), custom_call_target="tpu_custom_call" | custom-call | tf_op jit(solution)/shard_map/moe_block/pallas_call | solution.py:334
  69.5 1.6 %copy.11 = bf16[32,2048]{1,0:T(8,128)(2,1)} copy(bf16[32,2048]{1,0:T(8,128)(2,1)} %moe_block.1) | data formatting | bytes 262144

commit v5 on v4

--- a/solution.py
+++ b/solution.py
@@ -12,7 +12,7 @@
 LIMIT = 7.0
 ALPHA = 1.702
 MESH = pl.DeviceIdType.MESH
-PIECES = 8
+PIECES = 4
 STEPS = 4
 F32 = jnp.float32
 BF16 = jnp.bfloat16
@@ -40,6 +40,7 @@
     pair, zin = lax.rem(z, 2), lax.div(z, 2)
     partner, ypeer, zpeer = me + 1 - 2 * c, me + 2 - 4 * y, me + 8 - 16 * zin
     zfar = [me + 4 * (2 * j + 1 - pair - z) for j in range(2)]
+    is_mid = zin != pair
 
     def pos(q, cc, yy, zz):
         return ((q * 2 + cc) * 2 + yy) * 2 + zz
@@ -68,7 +69,7 @@
     pl.semaphore_wait(barrier, 5)
 
     TO_Z, TO_Y, TO_C, TO_F0, TO_F1 = range(5)
-    dest = [zpeer, ypeer, partner, zfar[0], zfar[1]]
+    dest = [zpeer, ypeer, partner, me + 4 * (2 * zin + 1 - pair - z), me + 4 * (3 - 2 * zin - pair - z)]
 
     def h_copy(b, d, s):
         rs = pl.ds(b * tok + s * half, half)
@@ -102,9 +103,8 @@
 
     near = pos(pair, c, y, 1 - zin)
     y_own, y_near = pos(pair, c, 1 - y, zin), pos(pair, c, 1 - y, 1 - zin)
-    first = lax.div(z, 3)
-    far = [pos(1 - pair, c, y, j) for j in (first, 1 - first)]
-    y_far = [pos(1 - pair, c, 1 - y, j) for j in (first, 1 - first)]
+    far = [pos(1 - pair, c, y, j) for j in (zin, 1 - zin)]
+    y_far = [pos(1 - pair, c, 1 - y, j) for j in (zin, 1 - zin)]
 
     for s in range(2):
         send_h(own, s, TO_Z, TO_Y)
@@ -121,9 +121,15 @@
     weight = jnp.where(chosen, jnp.exp(jnp.where(chosen, logits - top, 0.0)), 0.0)
     gates = jnp.where(chosen, weight / jnp.sum(weight, axis=-1, keepdims=True), -1.0)
     gate[pl.ds(own * tok, tok), :] = jnp.concatenate([gates, jnp.full((tok, 128 - experts), -1.0, F32)], axis=1)
-    send_g(own, TO_Z, TO_Y, TO_C, TO_F0, TO_F1)
-    for s in range(2):
-        send_h(own, s, TO_F0, TO_F1)
+    send_g(own, TO_Z, TO_Y, TO_C, TO_F0)
+    for s in range(2):
+        send_h(own, s, TO_F0)
+
+    @pl.when(is_mid)
+    def _():
+        send_g(own, TO_F1)
+        for s in range(2):
+            send_h(own, s, TO_F1)
 
     bgu[...] = bgu_ref[...].astype(F32)
     bd[...] = bd_ref[...].astype(F32)
@@ -135,6 +141,12 @@
         pass_h(y_own, s, TO_C)
     pass_g(near, TO_Y, TO_C)
     pass_g(y_own, TO_C)
+
+    @pl.when(is_mid)
+    def _():
+        send_g(near, TO_F0)
+        for s in range(2):
+            send_h(near, s, TO_F0)
     for s in range(2):
         pass_h(y_near, s, TO_C)
     pass_g(y_near, TO_C)
@@ -252,13 +264,16 @@
         out_ref[:, cols] = (x_ref[:, cols].astype(F32) + total).astype(BF16)
 
     finish_gather(pair)
+    forward_far(0)
     route(pair)
 
     for e in range(local_exp):
         w_copy(e).wait()
         gate_up(e, pair)
-        if e < 2:
-            forward_far(e)
+        if e == 1:
+            forward_far(1)
+        if e == 3:
+            forward_far_y(0)
     for i in range(local_exp, 2 * local_exp):
         w_copy(i).wait()
 
@@ -270,11 +285,7 @@
         def _():
             after_core(0, n - 1)
 
-        @pl.when(n == 1)
-        def _():
-            forward_far_y(0)
-
-        @pl.when(n == 3)
+        @pl.when(n == 2)
         def _():
             forward_far_y(1)
         return 0
@@ -285,8 +296,9 @@
     route(1 - pair)
     for e in range(local_exp):
         gate_up(e, 1 - pair)
-        for i in range(per):
-            after_y(0, e * per + i)
+        if e % 2 == 1:
+            for i in range(per):
+                after_y(0, (e // 2) * per + i)
 
     def down1(n, _):
         down(n, 1)
@@ -295,15 +307,27 @@
         @pl.when(n > 0)
         def _():
             after_core(1, n - 1)
+
+        @pl.when(n == 2)
+        def _():
+            for i in range(per):
+                after_y(0, 2 * per + i)
         return 0
     lax.fori_loop(0, STEPS, down1, 0)
     after_core(1, STEPS - 1)
+    for i in range(per):
+        after_y(0, 3 * per + i)
     for n in range(PIECES):
         after_y(1, n)
     for n in range(PIECES):
         finish(n)
 
-    sent(own, TO_Z, TO_Y, TO_C, TO_F0, TO_F1)
+    sent(own, TO_Z, TO_Y, TO_C, TO_F0)
+
+    @pl.when(is_mid)
+    def _():
+        sent(own, TO_F1)
+        sent(near, TO_F0)
     for b in (near, *far):
         sent(b, TO_Y, TO_C)
     for b in (y_own, y_near, *y_far):

time: 71.2 us -> 64.7 us (0.909)
  Pallas kernels: 69.5 us -> 63 us
    pallas_call x1, Pallas kernels: 69.5 us -> 63 us  [local_block(): pl.pallas_call(functools.partial(moe_kernel, cfg), out_shape=jax.ShapeDty...]
where the time goes in v5:
time: 64.7 us; the launch traced here: 64.6 us
  Pallas kernels  63 us (97%)
  local copies, waits for them, and re-layouts  1.57 us (2%)
    pallas_call x1, Pallas kernels, local_block(): pl.pallas_call(functools.partial(moe_kernel, cfg), out_shape=jax.ShapeDty...  63 us
    unnamed x1, local copies, waits for them, and re-layouts  1.57 us

profile of v5, /device:TPU:0, one launch (start us, length us, event | category | flops | bytes accessed | tf_op | source)
XLA Modules:
  0.0 64.6 jit_solution(5758022013827300080)
XLA Ops:
  0.0 63.0 %moe_block.1 = bf16[32,2048]{1,0:T(8,128)(2,1)} custom-call(bf16[32,2048]{1,0:T(8,128)(2,1)} %x_ref.1, s32[8,32]{1,0:T(8,128)} %bitcast.4, bf16[2048]{0:T(1024)(128)(2,1)} %g_ref.1, bf16[64,2048]{1,0:T(8,128)(2,1)} %bitcast.3, bf16[1,64]{1,0:T(2,128)(2,1)} %bitcast.5, bf16[4,2048,2048]{2,1,0:T(8,128)(2,1)} %wgu_hbm.1, bf16[4,2048]{1,0:T(4,128)(2,1)} %bgu_ref.1, ...), custom_call_target="tpu_custom_call" | custom-call | tf_op jit(solution)/shard_map/moe_block/pallas_call | solution.py:358
  63.0 1.6 %copy.11 = bf16[32,2048]{1,0:T(8,128)(2,1)} copy(bf16[32,2048]{1,0:T(8,128)(2,1)} %moe_block.1) | data formatting | bytes 262144

commit v6 on v5

--- a/solution.py
+++ b/solution.py
@@ -76,7 +76,7 @@
         return remote(hid.at[rs], hid.at[rs], s_h.at[d, b, s], q_h.at[b, s], dest[d])
 
     def g_copy(b, d):
-        rs = pl.ds(b * tok, tok)
+        rs = pl.ds(b * half, half)
         return remote(gate.at[rs], gate.at[rs], s_g.at[d, b], q_g.at[b], dest[d])
 
     def send_h(b, s, *ds):
@@ -120,7 +120,7 @@
     top = jnp.max(jnp.where(chosen, logits, -jnp.inf), axis=-1, keepdims=True)
     weight = jnp.where(chosen, jnp.exp(jnp.where(chosen, logits - top, 0.0)), 0.0)
     gates = jnp.where(chosen, weight / jnp.sum(weight, axis=-1, keepdims=True), -1.0)
-    gate[pl.ds(own * tok, tok), :] = jnp.concatenate([gates, jnp.full((tok, 128 - experts), -1.0, F32)], axis=1)
+    gate[pl.ds(own * half, half), :] = jnp.concatenate([gates[:half], gates[half:]], axis=1)
     send_g(own, TO_Z, TO_Y, TO_C, TO_F0)
     for s in range(2):
         send_h(own, s, TO_F0)
@@ -170,7 +170,8 @@
             pass_h(y_far[j], s, TO_C)
 
     def route(q):
-        g = gate[pl.ds(q * tc, tc), :]
+        g2 = gate[pl.ds(q * 8 * half, 8 * half), :]
+        g = jnp.concatenate([g2.reshape(8, half, 128), pltpu.roll(g2, experts, 1).reshape(8, half, 128)], axis=1).reshape(tc, 128)
         hit = g >= 0.0
         ri, rj = iota((tc, tc), 0), iota((tc, tc), 1)
         before = jnp.logical_and(rj < ri, lax.div(rj, tok) == lax.div(ri, tok)).astype(F32).astype(BF16)
@@ -291,11 +292,12 @@
         return 0
     lax.fori_loop(0, STEPS, down0, 0)
 
-    after_core(0, STEPS - 1)
     finish_gather(1 - pair)
     route(1 - pair)
     for e in range(local_exp):
         gate_up(e, 1 - pair)
+        if e == 0:
+            after_core(0, STEPS - 1)
         if e % 2 == 1:
             for i in range(per):
                 after_y(0, (e // 2) * per + i)
@@ -364,7 +366,7 @@
                 pltpu.VMEM((local_exp, d_model, 2 * d_ff), BF16),
                 pltpu.VMEM((local_exp, d_ff, d_model), BF16),
                 pltpu.VMEM((n_group * tok, d_model), BF16),
-                pltpu.VMEM((n_group * tok, 128), F32),
+                pltpu.VMEM((n_group * tok // 2, 2 * experts), F32),
                 pltpu.VMEM((local_exp * ns, tc), BF16),
                 pltpu.VMEM((tc, local_exp * ns), BF16),
                 pltpu.VMEM((tc, local_exp * 128), F32),

time: 64.7 us -> 63.8 us (0.986)
  Pallas kernels: 63 us -> 62.1 us
    pallas_call x1, Pallas kernels: 63 us -> 62.1 us  [local_block(): pl.pallas_call(functools.partial(moe_kernel, cfg), out_shape=jax.ShapeDty...]
where the time goes in v6:
time: 63.8 us; the launch traced here: 63.7 us
  Pallas kernels  62.1 us (97%)
  local copies, waits for them, and re-layouts  1.57 us (2%)
    pallas_call x1, Pallas kernels, local_block(): pl.pallas_call(functools.partial(moe_kernel, cfg), out_shape=jax.ShapeDty...  62.1 us
    unnamed x1, local copies, waits for them, and re-layouts  1.57 us

profile of v6, /device:TPU:0, one launch (start us, length us, event | category | flops | bytes accessed | tf_op | source)
XLA Modules:
  0.0 63.7 jit_solution(2770493196643223570)
XLA Ops:
  0.0 62.1 %moe_block.1 = bf16[32,2048]{1,0:T(8,128)(2,1)} custom-call(bf16[32,2048]{1,0:T(8,128)(2,1)} %x_ref.1, s32[8,32]{1,0:T(8,128)} %bitcast.4, bf16[2048]{0:T(1024)(128)(2,1)} %g_ref.1, bf16[64,2048]{1,0:T(8,128)(2,1)} %bitcast.3, bf16[1,64]{1,0:T(2,128)(2,1)} %bitcast.5, bf16[4,2048,2048]{2,1,0:T(8,128)(2,1)} %wgu_hbm.1, bf16[4,2048]{1,0:T(4,128)(2,1)} %bgu_ref.1, ...), custom_call_target="tpu_custom_call" | custom-call | tf_op jit(solution)/shard_map/moe_block/pallas_call | solution.py:360
  62.1 1.6 %copy.11 = bf16[32,2048]{1,0:T(8,128)(2,1)} copy(bf16[32,2048]{1,0:T(8,128)(2,1)} %moe_block.1) | data formatting | bytes 262144

commit v7 on v6

--- a/solution.py
+++ b/solution.py
@@ -222,14 +222,15 @@
     def core_copy(k, n):
         return remote(acc.at[k, n, pl.ds((1 - c) * 4 * tok, 4 * tok)], r_core.at[k, n], s_core.at[k, n], q_core.at[k, n], partner)
 
-    def y_copy(k, n):
-        return remote(acc.at[k, n, pl.ds((c * 2 + 1 - y) * 2 * tok, 2 * tok)], r_y.at[k, n], s_y.at[k, n], q_y.at[k, n], ypeer)
+    def y_copy(k, n, j):
+        return remote(acc.at[k, n, pl.ds(((c * 2 + 1 - y) * 2 + j) * tok, tok)], r_y.at[k, n, pl.ds(j * tok, tok)],
+                      s_y.at[k, n, j], q_y.at[k, n, j], ypeer)
 
     def near_copy(n):
         return remote(acc.at[0, n, pl.ds(mine + (1 - zin) * tok, tok)], r_z.at[2, n], s_z.at[2, n], q_z.at[2, n], zpeer)
 
     def far_copy(j, n):
-        return remote(acc.at[1, n, pl.ds(mine + j * tok, tok)], r_z.at[zin, n], s_z.at[j, n], q_z.at[zin, n], zfar[j])
+        return remote(acc.at[1, n, pl.ds(mine + j * tok, tok)], r_z.at[zin, n], s_z.at[j, n], q_z.at[zin, n], me + 4 * (2 * j + 1 - pair - z))
 
     def far_wait(j, n):
         remote(acc.at[1, n, pl.ds(mine + j * tok, tok)], r_z.at[j, n], s_z.at[j, n], q_z.at[j, n], zfar[j]).wait_recv()
@@ -243,17 +244,18 @@
             n = m * per + i
             core_copy(k, n).wait_recv()
             acc[k, n, pl.ds((c * 2 + 1 - y) * 2 * tok, 2 * tok)] += r_core[k, n, pl.ds((1 - y) * 2 * tok, 2 * tok)]
-            y_copy(k, n).start()
+            for j in (1 - zin, zin):
+                y_copy(k, n, j).start()
             acc[k, n, pl.ds(mine, 2 * tok)] += r_core[k, n, pl.ds(y * 2 * tok, 2 * tok)]
 
     def after_y(k, n):
-        y_copy(k, n).wait_recv()
-        acc[k, n, pl.ds(mine, 2 * tok)] += r_y[k, n]
-        if k == 0:
-            near_copy(n).start()
-        else:
-            for j in range(2):
+        for i, j in enumerate((1 - zin, zin)):
+            y_copy(k, n, j).wait_recv()
+            acc[k, n, pl.ds(mine + j * tok, tok)] += r_y[k, n, pl.ds(j * tok, tok)]
+            if k == 1:
                 far_copy(j, n).start()
+            elif i == 0:
+                near_copy(n).start()
 
     def finish(n):
         near_copy(n).wait_recv()
@@ -337,7 +339,8 @@
     for n in range(PIECES):
         for k in range(2):
             core_copy(k, n).wait_send()
-            y_copy(k, n).wait_send()
+            for j in range(2):
+                y_copy(k, n, j).wait_send()
             far_copy(k, n).wait_send()
         near_copy(n).wait_send()
 
@@ -382,7 +385,7 @@
                 pltpu.VMEM((3, PIECES, tok, cw), F32),
                 dma((2 * local_exp,)),
                 dma((5, n_group, 2)), dma((n_group, 2)), dma((5, n_group)), dma((n_group,)),
-                dma((2, PIECES)), dma((2, PIECES)), dma((2, PIECES)), dma((2, PIECES)),
+                dma((2, PIECES)), dma((2, PIECES)), dma((2, PIECES, 2)), dma((2, PIECES, 2)),
                 dma((3, PIECES)), dma((3, PIECES)),
             ],
             compiler_params=pltpu.CompilerParams(

time: 63.8 us -> 64 us (level)
  no operation moved by 1% of the time
where the time goes in v7:
time: 64 us; the launch traced here: 63.9 us
  Pallas kernels  62.3 us (97%)
  local copies, waits for them, and re-layouts  1.57 us (2%)
    pallas_call x1, Pallas kernels, local_block(): pl.pallas_call(functools.partial(moe_kernel, cfg), out_shape=jax.ShapeDty...  62.3 us
    unnamed x1, local copies, waits for them, and re-layouts  1.57 us

profile of v7, /device:TPU:0, one launch (start us, length us, event | category | flops | bytes accessed | tf_op | source)
XLA Modules:
  0.0 63.9 jit_solution(2800078096280355088)
XLA Ops:
  0.0 62.3 %moe_block.1 = bf16[32,2048]{1,0:T(8,128)(2,1)} custom-call(bf16[32,2048]{1,0:T(8,128)(2,1)} %x_ref.1, s32[8,32]{1,0:T(8,128)} %bitcast.4, bf16[2048]{0:T(1024)(128)(2,1)} %g_ref.1, bf16[64,2048]{1,0:T(8,128)(2,1)} %bitcast.3, bf16[1,64]{1,0:T(2,128)(2,1)} %bitcast.5, bf16[4,2048,2048]{2,1,0:T(8,128)(2,1)} %wgu_hbm.1, bf16[4,2048]{1,0:T(4,128)(2,1)} %bgu_ref.1, ...), custom_call_target="tpu_custom_call" | custom-call | tf_op jit(solution)/shard_map/moe_block/pallas_call | solution.py:363
  62.3 1.6 %copy.11 = bf16[32,2048]{1,0:T(8,128)(2,1)} copy(bf16[32,2048]{1,0:T(8,128)(2,1)} %moe_block.1) | data formatting | bytes 262144
